TPU v7x, 32 devices: a whole 2x2x4 slice. The times are simulated.
32 devices in a mesh: dp: 2 (over x), b: 4 (over z), cp: 4 (over y, core).
Axes of the slice: x: 2, y: 2, z: 4, core: 2. Of those that a mesh axis runs over, the one named last changes fastest.
Arguments:
- x: bfloat16 [8, 4096, 2048], P(('dp', 'b'), 'cp'), parts along dimension 0
- ids: int32 [8, 4096, 6], P(('dp', 'b'), 'cp'), parts along dimension 0
- g_attn: bfloat16 [2048], replicated
- w_q: bfloat16 [2048, 3072], replicated
- w_dkv: bfloat16 [2048, 512], replicated
- w_kr: bfloat16 [2048, 64], replicated
- w_uk: bfloat16 [16, 128, 512], replicated
- w_uv: bfloat16 [16, 512, 128], replicated
- w_o: bfloat16 [2048, 2048], replicated
- g_ffn: bfloat16 [2048], replicated
- w_fg: bfloat16 [2048, 11264], replicated
- w_fu: bfloat16 [2048, 11264], replicated
- w_fd: bfloat16 [11264, 2048], replicated
- g_moe: bfloat16 [2048], replicated
- w_r: bfloat16 [2048, 96], replicated
- w_eg: bfloat16 [64, 2048, 1408], P(('b', 'cp'))
- w_eu: bfloat16 [64, 2048, 1408], P(('b', 'cp'))
- w_ed: bfloat16 [64, 1408, 2048], P(('b', 'cp'))
Outputs:
- output: bfloat16 [8, 4096, 2048], P(('dp', 'b'), 'cp'), parts along dimension 0
There are 2 independent parts. A program takes and returns all parts, laid end to end along the dimension named above; an argument that names none is the same for every part.
All inputs are finite; a program needn't handle non-finite values.
Results may differ from a plain program's by a relative error of at most 0.00887259.
Values are sent between devices in bfloat16 or wider.
A program may use at most 1 GiB of HBM per device.

v0:
```python
import jax
import jax.numpy as jnp
from jax import lax
from jax.sharding import PartitionSpec as P

NOPE = 128
ROPE = 64
EPS = 1e-6
SCALE = (NOPE + ROPE) ** -0.5
F32 = jnp.float32
BF16 = jnp.bfloat16


def _rms(v, g):
    vf = v.astype(F32)
    return (vf * lax.rsqrt(jnp.mean(vf * vf, axis=-1, keepdims=True) + EPS) * g.astype(F32)).astype(BF16)


def _rope(v, cos, sin):
    half = ROPE // 2
    v1 = v[..., :half]
    v2 = v[..., half:]
    return jnp.concatenate([v1 * cos - v2 * sin, v1 * sin + v2 * cos], axis=-1)


def _swiglu(z, wg, wu, wd):
    hid = jax.nn.silu(jnp.dot(z, wg, preferred_element_type=F32)) * jnp.dot(z, wu, preferred_element_type=F32)
    return jnp.dot(hid.astype(BF16), wd, preferred_element_type=F32).astype(BF16)


def _prep(x, pos, g_attn, w_q, w_dkv, w_kr, w_uk):
    rows, seq, _ = x.shape
    heads = w_uk.shape[0]
    half = ROPE // 2
    ang = pos.astype(F32)[:, None] * (10000.0 ** (-jnp.arange(half, dtype=F32) / half))[None, :]
    cos = jnp.cos(ang)
    sin = jnp.sin(ang)
    n = _rms(x, g_attn)
    c = jnp.einsum('bsd,dr->bsr', n, w_dkv, preferred_element_type=F32).astype(BF16)
    kr = _rope(jnp.einsum('bsd,de->bse', n, w_kr, preferred_element_type=F32), cos, sin).astype(BF16)
    q = jnp.einsum('bsd,dk->bsk', n, w_q, preferred_element_type=F32).reshape(rows, seq, heads, NOPE + ROPE)
    qt = jnp.einsum('bshn,hnr->bhsr', q[..., :NOPE].astype(BF16), w_uk, preferred_element_type=F32).astype(BF16)
    qr = _rope(jnp.transpose(q[..., NOPE:], (0, 2, 1, 3)), cos, sin).astype(BF16)
    return jnp.concatenate([qt, qr], axis=-1), jnp.concatenate([c, kr], axis=-1)


def _update(state, qc, kv, mask):
    mx, den, acc = state
    r = acc.shape[-1]
    sc = jnp.einsum('bhqe,bke->bhqk', qc, kv, preferred_element_type=F32) * SCALE
    if mask is not None:
        sc = jnp.where(mask, sc, -jnp.inf)
    new = jnp.maximum(mx, jnp.max(sc, axis=-1))
    corr = jnp.exp(mx - new)
    p = jnp.exp(sc - new[..., None])
    den = den * corr + jnp.sum(p, axis=-1)
    pv = jnp.einsum('bhqk,bkr->bhqr', p.astype(BF16), kv[..., :r], preferred_element_type=F32)
    acc = acc * corr[..., None] + pv
    return new, den, acc


def _finish(state, w_uv, w_o):
    _, den, acc = state
    heads, r, vd = w_uv.shape
    lat = (acc / den[..., None]).astype(BF16)
    o = jnp.einsum('bhqr,hrv->bhqv', lat, w_uv, preferred_element_type=F32).astype(BF16)
    return jnp.einsum('cirw,iwe->cre', o, w_o.reshape(heads, vd, -1), preferred_element_type=F32).astype(BF16)


def _gates(u, ids, w_r):
    g = jax.nn.softmax(jnp.dot(u, w_r, preferred_element_type=F32), axis=-1)
    hit = ids[:, :, None] == jnp.arange(g.shape[1], dtype=ids.dtype)
    sel = jnp.sum(jnp.where(hit, g[:, None, :], 0.0), axis=2)
    return sel / jnp.sum(sel, axis=1, keepdims=True)


def _route(lab, gate, ne, cap):
    t = lab.shape[0]
    oh = lab[:, :, None] == jnp.arange(ne, dtype=lab.dtype)
    hit = jnp.any(oh, axis=1)
    ge = jnp.sum(jnp.where(oh, gate[:, :, None], 0.0), axis=1)
    k = jnp.arange(t)
    tri = (k[:, None] > k[None, :]).astype(BF16)
    pre = jnp.dot(tri, hit.astype(BF16), preferred_element_type=F32).astype(lab.dtype)
    sel = hit[:, :, None] & (pre[:, :, None] == jnp.arange(cap, dtype=lab.dtype))
    return sel, jnp.where(sel, ge[:, :, None], 0.0)


def _dispatch(u, sel):
    a = sel.reshape(sel.shape[0], -1).astype(BF16)
    return jnp.einsum('tp,td->pd', a, u, preferred_element_type=F32).astype(BF16)


def _experts(xs, w_eg, w_eu, w_ed):
    hid = (jax.nn.silu(jnp.einsum('gecd,edf->egcf', xs, w_eg, preferred_element_type=F32))
           * jnp.einsum('gecd,edf->egcf', xs, w_eu, preferred_element_type=F32))
    return jnp.einsum('egcf,efd->gecd', hid.astype(BF16), w_ed, preferred_element_type=F32).astype(BF16)


def _combine(ret, u, ids, gate, w, ne):
    zero = jnp.sum(jnp.where(ids >= ne, gate, 0.0), axis=1)
    hi = w.astype(BF16)
    r1 = w - hi.astype(F32)
    mid = r1.astype(BF16)
    lo = (r1 - mid.astype(F32)).astype(BF16)
    part = jnp.einsum('xtp,pd->xtd', jnp.stack([hi, mid, lo]), ret, preferred_element_type=F32)
    return zero[:, None] * u.astype(F32) + jnp.sum(part, axis=0)


def solution(mesh):
    ncp = mesh.shape['cp']
    ngroup = mesh.shape['b'] * ncp
    axes = ('b', 'cp')
    tok = P(('dp', 'b'), 'cp', None)
    rep = P()
    espec = P(('b', 'cp'), None, None)

    def body(x, ids, g_attn, w_q, w_dkv, w_kr, w_uk, w_uv, w_o, g_ffn, w_fg, w_fu, w_fd, g_moe, w_r, w_eg, w_eu, w_ed):
        rows, seq, d = x.shape
        heads, r, _ = w_uv.shape
        top = ids.shape[-1]
        t = rows * seq
        epd = w_eg.shape[0]
        ne = epd * ngroup
        hot = (w_r.shape[1] // top) // 2
        cap = (t + hot - 1) // hot
        i = lax.axis_index('cp')
        loc = jnp.arange(seq)
        qc, kv = _prep(x, i * seq + loc, g_attn, w_q, w_dkv, w_kr, w_uk)
        state = (jnp.full((rows, heads, seq), -jnp.inf, F32), jnp.zeros((rows, heads, seq), F32), jnp.zeros((rows, heads, seq, r), F32))
        state = _update(state, qc, kv, (loc[:, None] >= loc[None, :])[None, None])
        perm = [(k, (k + 1) % ncp) for k in range(ncp)]
        cur = kv
        for step in range(1, ncp):
            cur = lax.ppermute(cur, 'cp', perm)
            state = lax.cond((i - step) % ncp < i,
                             lambda st, kb: _update(st, qc, kb, None),
                             lambda st, kb: st, state, cur)
        a = _finish(state, w_uv, w_o)
        y = (x.astype(F32) + a.astype(F32)).astype(BF16).reshape(t, d)
        f = _swiglu(_rms(y, g_ffn), w_fg, w_fu, w_fd)
        u = _rms(x, g_moe).reshape(t, d)
        idf = ids.reshape(t, top)
        gate = _gates(u, idf, w_r)
        sel, w = _route(idf, gate, ne, cap)
        send = _dispatch(u, sel).reshape(ngroup, epd * cap, d)
        recv = lax.all_to_all(send, axes, 0, 0)
        out = _experts(recv.reshape(ngroup, epd, cap, d), w_eg, w_eu, w_ed)
        ret = lax.all_to_all(out, axes, 0, 0).reshape(ne * cap, d)
        m = _combine(ret, u, idf, gate, w.reshape(t, -1), ne)
        h = y.astype(F32) + f.astype(F32) + m
        return h.astype(BF16).reshape(rows, seq, d)

    return jax.shard_map(body, mesh=mesh, in_specs=(tok, tok) + (rep,) * 13 + (espec,) * 3, out_specs=tok, check_vma=False)
```

profile of v0, /device:TPU:15, one launch (start us, length us, event | category | flops | bytes accessed | tf_op | source)
XLA Modules:
  0.0 2070.1 jit_solution(5129982164810123458)
XLA Ops:
  0.0 0.9 copy.134
  0.9 0.6 copy-done.11
  1.7 0.6 fusion.125
  2.8 0.7 convert_element_type.247
  3.5 3.1 fusion.83
  6.6 20.7 fusion.54
  27.3 43.6 %fusion.59 = bf16[8192,2048]{1,0:T(8,128)(2,1)} fusion(pred[128,8,64,128]{3,2,1,0:T(32,128)(4,1)} %bitcast.256, bf16[1,1024,2048]{2,1,0:T(8,128)(2,1)} %param.24, f32[2048]{0:T(1024)S(1)} %convert_element_type.247, f32[1024]{0:T(1024)S(1)} %add_rsqrt_fusion.1), kind=kOutput, calls=%fused_computation.81 | convolution fusion | flops 34384904192 | bytes 46149632 | tf_op jit(solution)/shard_map/tp,td->pd/dot_general | solution.py:91
  70.9 7.1 all-to-all-start
  78.1 3.6 fusion.122
  81.8 0.6 fusion.134
  82.4 5.4 fusion.114
  87.8 1.1 copy-done.9
  88.8 1.1 pad_maximum_fusion.1
  89.9 0.6 collective-permute-start
  90.5 710.0 %all-to-all-done = bf16[16,512,2048]{2,1,0:T(8,128)(2,1)} async-done(((bf16[16,512,2048]{2,1,0:T(8,128)(2,1)}), bf16[16,512,2048]{2,1,0:T(8,128)(2,1)}, u32[]{:S(2)}, u32[]{:S(2)}) %all-to-all-start) | async-done | bytes 33554464 | tf_op jit(solution)/shard_map/all_to_all | solution.py:147
  800.5 62.2 %fusion.63 = f32[4,16,128,1408]{3,2,1,0:T(8,128)} fusion(bf16[16,4,128,2048]{3,2,1,0:T(8,128)(2,1)} %bitcast.62, bf16[4,2048,1408]{2,1,0:T(8,128)(2,1)} %param.39), kind=kOutput, calls=%fused_computation.83 | convolution fusion | flops 47244640256 | bytes 102760448 | tf_op jit(solution)/shard_map/gecd,edf->egcf/dot_general | solution.py:95
  862.7 76.8 %multiply_convert_fusion = bf16[4,16,128,1408]{3,2,1,0:T(8,128)(2,1)} fusion(f32[4,16,128,1408]{3,2,1,0:T(8,128)} %fusion.63, bf16[16,4,128,2048]{3,2,1,0:T(8,128)(2,1)} %bitcast.62, bf16[4,2048,1408]{2,1,0:T(8,128)(2,1)} %param.40), kind=kOutput, calls=%fused_computation.63 | convolution fusion | flops 47313846272 | bytes 125829120 | tf_op jit(solution)/shard_map/gecd,edf->egcf/dot_general | solution.py:96
  939.5 60.6 %convert_bitcast_fusion = bf16[16,4,128,2048]{3,2,0,1:T(8,128)(2,1)} fusion(bf16[4,16,128,1408]{3,2,1,0:T(8,128)(2,1)} %multiply_convert_fusion, bf16[4,1408,2048]{2,1,0:T(8,128)(2,1)} %param.41), kind=kOutput, calls=%fused_computation.66 | convolution fusion | flops 47261417472 | bytes 79691776 | tf_op jit(solution)/shard_map/egcf,efd->gecd/dot_general | solution.py:97
  1000.1 22.9 %copy.100 = bf16[16,4,128,2048]{3,2,1,0:T(8,128)(2,1)} copy(bf16[16,4,128,2048]{3,2,0,1:T(8,128)(2,1)} %convert_bitcast_fusion) | data formatting | bytes 67108864 | tf_op jit(solution)/shard_map/convert_element_type | solution.py:97
  1023.1 6.3 all-to-all-start.1
  1029.5 3.7 fusion.148
  1033.8 0.6 select_reduce_fusion.3
  1034.8 21.5 %broadcast_in_dim.74 = f32[1024,64,128]{2,1,0:T(8,128)} broadcast(f32[1024,64]{1,0:T(8,128)S(1)} %copy.97), dimensions={0,1} | broadcast | bytes 33816576 | tf_op jit(solution)/shard_map/jit(_where)/broadcast_in_dim | solution.py:86
  1056.3 35.9 %broadcast_in_dim.75 = f32[1,1024,8192]{2,1,0:T(8,128)} reshape(f32[1024,64,128]{2,1,0:T(8,128)} %broadcast_in_dim.74) | data formatting | bytes 67108864 | tf_op jit(solution)/shard_map/jit(_where)/broadcast_in_dim | solution.py:86
  1092.2 12.0 and.55
  1104.2 22.9 %and.56 = pred[1,1024,8192]{2,1,0:T(8,128)(4,1)} reshape(pred[1024,64,128]{2,1,0:T(8,128)(4,1)} %and.55) | data formatting | bytes 16777216 | tf_op jit(solution)/shard_map/and | solution.py:85
  1127.1 11.8 eq.83
  1138.9 35.9 %eq.84 = s32[1,1024,8192]{2,1,0:T(8,128)} reshape(s32[1024,64,128]{2,1,0:T(8,128)} %eq.83) | data formatting | bytes 67108864 | tf_op jit(solution)/shard_map/eq | solution.py:85
  1174.8 16.3 copy.87
  1191.4 0.5 multiply_cosine_fusion.1
  1192.0 17.4 convolution_bitcast_fusion
  1209.4 4.5 copy-done.2
  1214.4 2.0 subtract_convert_fusion.1
  1216.4 11.7 convert_bitcast_fusion.1
  1228.1 35.4 %fusion.40 = (f32[16,1024]{1,0:T(8,128)S(1)}, f32[16,1024,1024]{1,2,0:T(8,128)}) fusion(pred[1024,1024]{0,1:T(8,128)(4,1)S(1)} %iota_compare_fusion.2, bf16[1,1024,32]{1,2,0:T(8,128)(2,1)S(1)} %copy-done.16, bf16[1,1024,32]{1,2,0:T(8,128)(2,1)S(1)} %copy-done.14, bf16[1,1024,512]{1,2,0:T(8,128)(2,1)} %bitcast.261, ...), kind=kOutput, calls=%fused_computation.54 | convolution fusion | flops 19437830144 | bytes 88276992 | tf_op jit(solution)/shard_map/bhqe,bke->bhqk/dot_general | solution.py:50
  1263.5 40.5 %fusion.147 = (bf16[1,1024,8192]{2,1,0:T(8,128)(2,1)}, f32[1,1024,8192]{2,1,0:T(8,128)}) fusion(f32[1,1024,8192]{2,1,0:T(8,128)} %broadcast_in_dim.75, pred[1,1024,8192]{2,1,0:T(8,128)(4,1)} %and.56, s32[1,1024,8192]{2,1,0:T(8,128)} %eq.84, s32[8192]{0:T(1024)S(1)} %iota_bitcast_fusion), kind=kLoop, calls=%fused_computation.177 | loop fusion | flops 33554432 | bytes 125861888 | tf_op jit(solution)/shard_map/convert_element_type | solution.py:102
  1304.0 42.8 %add_bitcast_fusion = f32[1,16,1024,512]{3,2,1,0:T(8,128)} fusion(f32[16,1024]{1,0:T(8,128)S(1)} %exponential_multiply_fusion, f32[16,1024,1024]{1,2,0:T(8,128)} %get-tuple-element.171, f32[16,1024]{1,0:T(8,128)S(1)} %get-tuple-element.170, pred[1024,1024]{0,1:T(8,128)(4,1)S(1)} %iota_compare_fusion.2, bf16[1024,512]{0,1:T(8,128)(2,1)S(1)} %copy-done.10), kind=kOutput, calls=%fused_computation.71 | convolution fusion | flops 17255366656 | bytes 102891520 | tf_op jit(solution)/shard_map/bhqk,bkr->bhqr/dot_general | solution.py:57
  1346.8 21.6 %fusion.42 = f32[16,1024]{1,0:T(8,128)S(1)} fusion(f32[16,1024,1024]{1,2,0:T(8,128)} %get-tuple-element.171, f32[16,1024]{1,0:T(8,128)S(1)} %get-tuple-element.170, pred[1024,1024]{0,1:T(8,128)(4,1)S(1)} %iota_compare_fusion.2), kind=kLoop, calls=%fused_computation.56 | loop fusion | flops 67092480 | bytes 68288512 | tf_op jit(solution)/shard_map/reduce_sum | solution.py:56
  1368.5 35.1 %fusion.65 = (bf16[1,1024,8192]{2,1,0:T(8,128)(2,1)}, bf16[1,1024,8192]{2,1,0:T(8,128)(2,1)}) fusion(f32[1,1024,8192]{2,1,0:T(8,128)} %get-tuple-element.151), kind=kLoop, calls=%fused_computation.85 | loop fusion | flops 58720256 | bytes 67108864 | tf_op jit(solution)/shard_map/convert_element_type | solution.py:104
  1403.6 0.6 convert_element_type.242
  1404.2 2.5 collective-permute-start.2
  1406.7 18.5 pad_maximum_fusion
  1425.3 104.1 %conditional.3 = ((f32[1,16,1024]{2,1,0:T(8,128)S(1)}, f32[1,16,1024]{2,1,0:T(8,128)S(1)}, f32[1,16,1024,512]{3,2,1,0:T(8,128)})) conditional(s32[]{:T(128)} %convert_element_type.223, (f32[1,16,1024]{2,1,0:T(8,128)S(1)}, f32[1,16,1024]{2,1,0:T(8,128)S(1)}, f32[1,16,1024,512]{3,2,1,0:T(8,128)}) %tuple.73, (bf16[1,16,1024,576]{2,3,1,0:T(8,128)(2,1)}, ...), branch_computations={%region_3.4_spmd, %region_4.7_spmd} | conditional | flops 36658266112 | bytes 292945952 | solution.py:136
  1425.3 36.6 %multiply_reduce_fusion = (f32[16,1024]{1,0:T(8,128)S(1)}, f32[16,1024,1024]{1,2,0:T(8,128)}) fusion(bf16[1,16,1024,576]{2,3,1,0:T(8,128)(2,1)} %get-tuple-element.52, bf16[1,1024,576]{1,2,0:T(8,128)(2,1)} %get-tuple-element.128), kind=kOutput, calls=%fused_computation.1 | convolution fusion | flops 19360890880 | bytes 87228416 | tf_op jit(solution)/shard_map/cond/branch_1_fun/bhqe,bke->bhqk/dot_general | solution.py:50
  1461.9 21.4 %fusion.1 = f32[16,1024]{1,0:T(8,128)S(1)} fusion(f32[16,1024,1024]{1,2,0:T(8,128)} %get-tuple-element.157, f32[16,1024]{1,0:T(8,128)S(1)} %bitcast.262), kind=kLoop, calls=%fused_computation.3 | loop fusion | flops 50315264 | bytes 67239936 | tf_op jit(solution)/shard_map/cond/branch_1_fun/reduce_sum | solution.py:56
  1483.3 1.7 copy.92
  1485.0 44.0 %bitcast_add_fusion = f32[1,16,1024,512]{3,2,1,0:T(8,128)} fusion(f32[1,16,1024,512]{3,2,1,0:T(8,128)} %get-tuple-element.55, f32[16,1024]{1,0:T(8,128)S(1)} %get-tuple-element.144, f32[16,1024,1024]{1,2,0:T(8,128)} %get-tuple-element.157, f32[16,1024]{1,0:T(8,128)S(1)} %bitcast.263, bf16[1,1024,576]{2,1,0:T(8,128)(2,1)S(1)} %copy.92), kind=kOutput, calls=%fused_computation.5 | convolution fusion | flops 17246978048 | bytes 135397376 | tf_op jit(solution)/shard_map/cond/branch_1_fun/bhqk,bkr->bhqr/dot_general | solution.py:57
  1529.4 103.8 %conditional.4 = ((f32[1,16,1024]{2,1,0:T(8,128)S(1)}, f32[1,16,1024]{2,1,0:T(8,128)S(1)}, f32[1,16,1024,512]{3,2,1,0:T(8,128)})) conditional(s32[]{:T(128)} %convert_element_type.222, (f32[1,16,1024]{2,1,0:T(8,128)S(1)}, f32[1,16,1024]{2,1,0:T(8,128)S(1)}, f32[1,16,1024,512]{3,2,1,0:T(8,128)}) %get-tuple-element.190, ...), branch_computations={%region_7.8_spmd, %region_8.11_spmd} | conditional | flops 36658266112 | bytes 292945952 | solution.py:136
  1529.4 36.6 %multiply_reduce_fusion.1 = (f32[16,1024]{1,0:T(8,128)S(1)}, f32[16,1024,1024]{1,2,0:T(8,128)}) fusion(bf16[1,16,1024,576]{2,3,1,0:T(8,128)(2,1)} %get-tuple-element.57, bf16[1,1024,576]{1,2,0:T(8,128)(2,1)} %get-tuple-element.133), kind=kOutput, calls=%fused_computation.18 | convolution fusion | flops 19360890880 | bytes 87228416 | tf_op jit(solution)/shard_map/cond/branch_1_fun/bhqe,bke->bhqk/dot_general | solution.py:50
  1566.0 21.4 %fusion.14 = f32[16,1024]{1,0:T(8,128)S(1)} fusion(f32[16,1024,1024]{1,2,0:T(8,128)} %get-tuple-element.159, f32[16,1024]{1,0:T(8,128)S(1)} %bitcast.264), kind=kLoop, calls=%fused_computation.20 | loop fusion | flops 50315264 | bytes 67239936 | tf_op jit(solution)/shard_map/cond/branch_1_fun/reduce_sum | solution.py:56
  1587.5 1.7 copy.93
  1589.1 44.0 %bitcast_add_fusion.2 = f32[1,16,1024,512]{3,2,1,0:T(8,128)} fusion(f32[1,16,1024,512]{3,2,1,0:T(8,128)} %get-tuple-element.60, f32[16,1024]{1,0:T(8,128)S(1)} %get-tuple-element.146, f32[16,1024,1024]{1,2,0:T(8,128)} %get-tuple-element.159, f32[16,1024]{1,0:T(8,128)S(1)} %bitcast.265, bf16[1,1024,576]{2,1,0:T(8,128)(2,1)S(1)} %copy.93), kind=kOutput, calls=%fused_computation.22 | convolution fusion | flops 17246978048 | bytes 135397376 | tf_op jit(solution)/shard_map/cond/branch_1_fun/bhqk,bkr->bhqr/dot_general | solution.py:57
  1633.2 104.1 %conditional.5 = ((f32[1,16,1024]{2,1,0:T(8,128)S(1)}, f32[1,16,1024,512]{3,2,1,0:T(8,128)})) conditional(s32[]{:T(128)} %convert_element_type.221, (f32[1,16,1024]{2,1,0:T(8,128)S(1)}, f32[1,16,1024,512]{3,2,1,0:T(8,128)}) %tuple.28, (bf16[1,16,1024,576]{2,3,1,0:T(8,128)(2,1)}, bf16[1,1024,576]{1,2,0:T(8,128)(2,1)}, ...), branch_computations={%region_11.12_spmd, %region_12.15_spmd} | conditional | flops 36658282496 | bytes 292814848 | solution.py:136
  1633.3 36.6 %multiply_reduce_fusion.2 = (f32[16,1024]{1,0:T(8,128)S(1)}, f32[16,1024,1024]{1,2,0:T(8,128)}) fusion(bf16[1,16,1024,576]{2,3,1,0:T(8,128)(2,1)} %get-tuple-element.63, bf16[1,1024,576]{1,2,0:T(8,128)(2,1)} %get-tuple-element.138), kind=kOutput, calls=%fused_computation.35 | convolution fusion | flops 19360890880 | bytes 87228416 | tf_op jit(solution)/shard_map/cond/branch_1_fun/bhqe,bke->bhqk/dot_general | solution.py:50
  1669.9 21.4 %fusion.27 = f32[16,1024]{1,0:T(8,128)S(1)} fusion(f32[16,1024,1024]{1,2,0:T(8,128)} %get-tuple-element.155, f32[16,1024]{1,0:T(8,128)S(1)} %get-tuple-element.153), kind=kLoop, calls=%fused_computation.37 | loop fusion | flops 50315264 | bytes 67239936 | tf_op jit(solution)/shard_map/cond/branch_1_fun/reduce_sum | solution.py:56
  1691.4 1.7 copy.94
  1693.0 44.0 %bitcast_add_fusion.4 = f32[1,16,1024,512]{3,2,1,0:T(8,128)} fusion(f32[1,16,1024,512]{3,2,1,0:T(8,128)} %get-tuple-element.65, f32[16,1024]{1,0:T(8,128)S(1)} %get-tuple-element.152, f32[16,1024,1024]{1,2,0:T(8,128)} %get-tuple-element.155, f32[16,1024]{1,0:T(8,128)S(1)} %get-tuple-element.153, bf16[1,1024,576]{2,1,0:T(8,128)(2,1)S(1)} %copy.94), kind=kOutput, calls=%fused_computation.39 | convolution fusion | flops 17246978048 | bytes 135397376 | tf_op jit(solution)/shard_map/cond/branch_1_fun/bhqk,bkr->bhqr/dot_general | solution.py:57
  1737.3 15.7 fusion.112.clone.4
  1753.0 13.0 fusion.85
  1766.0 2.0 copy-done.36
  1768.0 54.5 %fusion.119 = f32[1024,11264]{1,0:T(8,128)} fusion(bf16[2048,11264]{1,0:T(8,128)(2,1)} %param.34, bf16[1024,2048]{1,0:T(8,128)(2,1)S(1)} %get-tuple-element.173, f32[2048]{0:T(1024)S(1)} %copy-done.23, f32[1024]{0:T(1024)S(1)} %add_rsqrt_fusion), kind=kOutput, calls=%fused_computation.141 | convolution fusion | flops 47253028864 | bytes 96481280 | tf_op jit(solution)/shard_map/dot_general | solution.py:27
  1822.5 63.7 %multiply_convert_fusion.1.clone.6 = bf16[1024,11264]{1,0:T(8,128)(2,1)} fusion(f32[1024,11264]{1,0:T(8,128)} %fusion.119, bf16[2048,11264]{1,0:T(8,128)(2,1)} %param.35, bf16[1024,2048]{1,0:T(8,128)(2,1)} %copy-done.36, f32[2048]{0:T(1024)S(1)} %copy-done.23, f32[1024]{0:T(1024)S(1)} %add_rsqrt_fusion), kind=kOutput, calls=%fused_computation.64.clone.clone.clone.clone.clone.1 | convolution fusion | flops 47322234880 | bytes 119549952 | tf_op jit(solution)/shard_map/dot_general | solution.py:27
  1886.3 122.3 %fusion.90 = f32[1024,2048]{1,0:T(8,128)} fusion(bf16[8192,2048,1]{1,0,2:T(8,128)(2,1)} %bitcast.71, bf16[1,1024,8192]{2,1,0:T(8,128)(2,1)} %get-tuple-element.161, bf16[1,1024,8192]{2,1,0:T(8,128)(2,1)} %get-tuple-element.160, bf16[1,1024,8192]{2,1,0:T(8,128)(2,1)} %get-tuple-element.150), kind=kOutput, calls=%fused_computation.116 | convolution fusion | flops 103133741056 | bytes 92274688 | tf_op jit(solution)/shard_map/xtp,pd->xtd/dot_general | solution.py:106
  2008.6 61.0 %fusion.95 = bf16[1,1024,2048]{2,1,0:T(8,128)(2,1)} fusion(f32[1024,2048]{1,0:T(8,128)} %fusion.90, bf16[1024,2048]{1,0:T(8,128)(2,1)} %copy-done.36, f32[1024]{0:T(1024)S(1)} %copy-done.28, bf16[11264,2048]{1,0:T(8,128)(2,1)} %param.36, f32[2048]{0:T(1024)S(1)} %copy-done.22, f32[1024]{0:T(1024)S(1)} %copy-done.31, bf16[1,1024,2048]{2,1,0:T(8,128)(2,1)} %param.24, ...), kind=kOutput, calls=%fused_computation.119 | convolution fusion | flops 47271903232 | bytes 90193920 | tf_op jit(solution)/shard_map/dot_general | solution.py:28
  (101 shorter events, 2.9 us)
Async XLA Ops:
  0.0 1216.4 %copy-start = (bf16[16,128,512]{2,1,0:T(8,128)(2,1)S(1)}, bf16[16,128,512]{2,1,0:T(8,128)(2,1)}, u32[]{:S(2)}) copy-start(bf16[16,128,512]{2,1,0:T(8,128)(2,1)} %param.30) | copy-start | bytes 6291460
  0.9 0.6 copy-start.11
  2.6 68.3 %copy-start.7 = (pred[1024,64]{1,0:T(8,128)(4,1)}, pred[1024,64]{1,0:T(8,128)(4,1)S(1)}, u32[]{:S(2)}) copy-start(pred[1024,64]{1,0:T(8,128)(4,1)S(1)} %copy.95) | copy-start | bytes 196612
  2.8 68.1 %copy-start.3 = (s32[1024,64]{1,0:T(8,128)}, s32[1024,64]{1,0:T(8,128)S(1)}, u32[]{:S(2)}) copy-start(s32[1024,64]{1,0:T(8,128)S(1)} %copy.96) | copy-start | bytes 786436
  3.5 67.4 %copy-start.20 = (f32[2048]{0:T(1024)}, f32[2048]{0:T(1024)S(1)}, u32[]{:S(2)}) copy-start(f32[2048]{0:T(1024)S(1)} %convert_element_type.247) | copy-start | bytes 24580
  6.6 75.7 %copy-start.29 = (f32[1024]{0:T(1024)}, f32[1024]{0:T(1024)S(1)}, u32[]{:S(2)}) copy-start(f32[1024]{0:T(1024)S(1)} %add_rsqrt_fusion.1) | copy-start | bytes 12292
  70.9 7.1 copy-start.26
  70.9 7.2 copy-start.35
  70.9 729.5 %all-to-all-start = ((bf16[16,512,2048]{2,1,0:T(8,128)(2,1)}), bf16[16,512,2048]{2,1,0:T(8,128)(2,1)}, u32[]{:S(2)}, u32[]{:S(2)}) async-start(bf16[16,512,2048]{2,1,0:T(8,128)(2,1)} %bitcast.254), calls=%async_computation | async-start | bytes 67108864 | tf_op jit(solution)/shard_map/all_to_all | solution.py:147
  78.0 9.7 copy-start.24
  78.1 9.7 copy-start.32
  78.1 3.7 copy-start.18
  82.3 7.6 copy-start.13
  82.3 7.6 copy-start.15
  87.8 1.1 copy-start.9
  89.9 1278.4 %collective-permute-start = (bf16[1,1024,576]{1,2,0:T(8,128)(2,1)}, bf16[1,1024,576]{1,2,0:T(8,128)(2,1)}, u32[]{:S(2)}, u32[]{:S(2)}) collective-permute-start(bf16[1,1024,576]{1,2,0:T(8,128)(2,1)} %pad_maximum_fusion.1), channel_id=1, source_target_pairs={{0,1},{1,2},{2,3},{3,0},{4,5},{5,6},{6,7},{7,4},{8,9},{9,10},{10,1... | collective-permute-start | bytes 3538952 | tf_op jit(solution)/shard_map/ppermute | solution.py:135
  1023.1 6.4 copy-start.21
  1023.1 6.4 copy-start.30
  1023.1 6.4 copy-start.34
  1023.1 10.3 copy-start.12
  1023.1 10.7 copy-start.17
  1023.1 863.1 %all-to-all-start.1 = ((bf16[16,4,128,2048]{3,2,1,0:T(8,128)(2,1)}), bf16[16,4,128,2048]{3,2,1,0:T(8,128)(2,1)}, u32[]{:S(2)}, u32[]{:S(2)}) async-start(bf16[16,4,128,2048]{3,2,1,0:T(8,128)(2,1)} %copy.100), calls=%async_computation.1 | async-start | bytes 67108864 | tf_op jit(solution)/shard_map/all_to_all | solution.py:149
  1056.3 35.9 %copy-start.8 = (pred[1024,64]{1,0:T(8,128)(4,1)S(1)}, pred[1024,64]{1,0:T(8,128)(4,1)}, u32[]{:S(2)}) copy-start(pred[1024,64]{1,0:T(8,128)(4,1)} %copy-done.7) | copy-start | bytes 196612
  1092.2 34.8 %copy-start.4 = (s32[1024,64]{1,0:T(8,128)S(1)}, s32[1024,64]{1,0:T(8,128)}, u32[]{:S(2)}) copy-start(s32[1024,64]{1,0:T(8,128)} %copy-done.3) | copy-start | bytes 786436
  1174.8 16.6 copy-start.19
  1174.8 16.7 copy-start.33
  1174.8 17.2 copy-start.25
  1209.4 4.5 copy-start.2
  1216.4 11.7 copy-start.14
  1216.4 11.7 copy-start.16
  1263.5 40.5 %copy-start.10 = (bf16[1024,512]{0,1:T(8,128)(2,1)S(1)}, bf16[1024,512]{0,1:T(8,128)(2,1)}, u32[]{:S(2)}) copy-start(bf16[1024,512]{0,1:T(8,128)(2,1)} %copy-done.9) | copy-start | bytes 3145732
  1368.4 35.9 %collective-permute-start.1 = (bf16[1,1024,576]{1,2,0:T(8,128)(2,1)}, bf16[1,1024,576]{1,2,0:T(8,128)(2,1)}, u32[]{:S(2)}, u32[]{:S(2)}) collective-permute-start(bf16[1,1024,576]{1,2,0:T(8,128)(2,1)} %collective-permute-done), channel_id=1, source_target_pairs={{0,1},{1,2},{2,3},{3,0},{4,5},{5,6},{6,7},{7,4},{8,9},{9,10},{10,1... | collective-permute-start | bytes 3538952 | tf_op jit(solution)/shard_map/ppermute | solution.py:135
  1368.4 35.2 %copy-start.27 = (bf16[2048]{0:T(1024)(128)(2,1)S(1)}, bf16[2048]{0:T(1024)(128)(2,1)}, u32[]{:S(2)}) copy-start(bf16[2048]{0:T(1024)(128)(2,1)} %param.33) | copy-start | bytes 12292
  1368.4 38.3 %copy-start.5 = (bf16[1,16,1024,32]{2,3,1,0:T(8,128)(2,1)S(1)}, bf16[1,16,1024,32]{2,3,1,0:T(8,128)(2,1)}, u32[]{:S(2)}) copy-start(bf16[1,16,1024,32]{2,3,1,0:T(8,128)(2,1)} %get-tuple-element.162) | copy-start | bytes 3145732
  1368.5 38.3 %copy-start.6 = (bf16[1,16,1024,32]{2,3,1,0:T(8,128)(2,1)S(1)}, bf16[1,16,1024,32]{2,3,1,0:T(8,128)(2,1)}, u32[]{:S(2)}) copy-start(bf16[1,16,1024,32]{2,3,1,0:T(8,128)(2,1)} %get-tuple-element.163) | copy-start | bytes 3145732
  1404.2 228.9 %collective-permute-start.2 = (bf16[1,1024,576]{1,2,0:T(8,128)(2,1)}, bf16[1,1024,576]{1,2,0:T(8,128)(2,1)}, u32[]{:S(2)}, u32[]{:S(2)}) collective-permute-start(bf16[1,1024,576]{1,2,0:T(8,128)(2,1)} %collective-permute-done.1), channel_id=1, source_target_pairs={{0,1},{1,2},{2,3},{3,0},{4,5},{5,6},{6,7},{7,4},{8,9},{9,10},{10,1... | collective-permute-start | bytes 3538952 | tf_op jit(solution)/shard_map/ppermute | solution.py:135
  1753.0 15.0 copy-start.23
  1766.0 2.0 copy-start.36
  1886.2 122.4 %copy-start.22 = (f32[2048]{0:T(1024)S(1)}, f32[2048]{0:T(1024)}, u32[]{:S(2)}) copy-start(f32[2048]{0:T(1024)} %copy-done.20) | copy-start | bytes 24580
  1886.2 122.4 %copy-start.28 = (f32[1024]{0:T(1024)S(1)}, f32[1024]{0:T(1024)}, u32[]{:S(2)}) copy-start(f32[1024]{0:T(1024)} %get-tuple-element.148) | copy-start | bytes 12292
  1886.2 122.3 %copy-start.31 = (f32[1024]{0:T(1024)S(1)}, f32[1024]{0:T(1024)}, u32[]{:S(2)}) copy-start(f32[1024]{0:T(1024)} %copy-done.29) | copy-start | bytes 12292
  2008.6 61.0 %copy-start.1 = (bf16[16,128,512]{2,1,0:T(8,128)(2,1)S(1)}, bf16[16,128,512]{2,1,0:T(8,128)(2,1)}, u32[]{:S(2)}) copy-start(bf16[16,128,512]{2,1,0:T(8,128)(2,1)} %param.30) | copy-start | bytes 6291460
where the time goes:
time: 2080 us; the launch traced here: 2070 us
  matrix products  936 us (45%)
  waiting for transfers between devices  710 us (34%)
  other arithmetic  211 us (10%)
  local copies, waits for them, and re-layouts  195 us (9%)
    all_to_all x1, waiting for transfers between devices, body(): recv = lax.all_to_all(send, axes, 0, 0)  710 us
    dot_general x4, matrix products, _update(): jnp.einsum('bhqk,bkr->bhqr', p.astype(BF16), kv[..., :r], preferred_eleme...  175 us
    dot_general x4, matrix products, _update(): jnp.einsum('bhqe,bke->bhqk', qc, kv, preferred_element_type=F32) * SCALE  145 us
    dot_general x1, matrix products, _combine(): jnp.einsum('xtp,pd->xtd', jnp.stack([hi, mid, lo]), ret, preferred_elemen...  122 us
    reduce_sum x4, other arithmetic, _update(): den = den * corr + jnp.sum(p, axis=-1)  85.6 us
    dot_general x1, matrix products, _experts(): jnp.einsum('gecd,edf->egcf', xs, w_eu, preferred_element_type=F32)  76.8 us
    dot_general x1, matrix products, _swiglu(): jnp.dot(z, wu, preferred_element_type=F32)  63.7 us
    dot_general x1, matrix products, _experts(): jnp.einsum('gecd,edf->egcf', xs, w_eg, preferred_element_type=F32)  62.2 us
  transfers between devices with their start and end apart: 5, of which 1 were waited for; matrix products, arithmetic and copies ran while one was open for 52% of the time, Pallas kernels for 0%

commit v1 on v0

v1 whole, which is shorter than its diff:
```python
import functools

import jax
import jax.numpy as jnp
from jax import lax
from jax.experimental import pallas as pl
from jax.experimental.pallas import tpu as pltpu
from jax.sharding import PartitionSpec as P

NOPE = 128
ROPE = 64
EPS = 1e-6
SCALE = (NOPE + ROPE) ** -0.5
F32 = jnp.float32
BF16 = jnp.bfloat16


def _rms(v, g):
    vf = v.astype(F32)
    return (vf * lax.rsqrt(jnp.mean(vf * vf, axis=-1, keepdims=True) + EPS) * g.astype(F32)).astype(BF16)


def _rope(v, cos, sin):
    half = ROPE // 2
    v1 = v[..., :half]
    v2 = v[..., half:]
    return jnp.concatenate([v1 * cos - v2 * sin, v1 * sin + v2 * cos], axis=-1)


def _swiglu(z, wg, wu, wd):
    hid = jax.nn.silu(jnp.dot(z, wg, preferred_element_type=F32)) * jnp.dot(z, wu, preferred_element_type=F32)
    return jnp.dot(hid.astype(BF16), wd, preferred_element_type=F32).astype(BF16)


def _prep(x, pos, g_attn, w_q, w_dkv, w_kr, w_uk):
    rows, seq, _ = x.shape
    heads = w_uk.shape[0]
    half = ROPE // 2
    ang = pos.astype(F32)[:, None] * (10000.0 ** (-jnp.arange(half, dtype=F32) / half))[None, :]
    cos = jnp.cos(ang)
    sin = jnp.sin(ang)
    n = _rms(x, g_attn)
    c = jnp.einsum('bsd,dr->bsr', n, w_dkv, preferred_element_type=F32).astype(BF16)
    kr = _rope(jnp.einsum('bsd,de->bse', n, w_kr, preferred_element_type=F32), cos, sin).astype(BF16)
    q = jnp.einsum('bsd,dk->bsk', n, w_q, preferred_element_type=F32).reshape(rows, seq, heads, NOPE + ROPE)
    qt = jnp.einsum('bshn,hnr->bhsr', q[..., :NOPE].astype(BF16), w_uk, preferred_element_type=F32).astype(BF16)
    qr = _rope(jnp.transpose(q[..., NOPE:], (0, 2, 1, 3)), cos, sin).astype(BF16)
    return jnp.concatenate([qt, qr], axis=-1), jnp.concatenate([c, kr], axis=-1)


LANES = 128


def _block_kernel(r, sub, first, q_ref, kv_ref, *refs):
    if first:
        mo_ref, lo_ref, ao_ref = refs
    else:
        m_ref, l_ref, a_ref, mo_ref, lo_ref, ao_ref = refs
    kv = kv_ref[0]
    tq = q_ref.shape[1]
    for n in range(tq // sub):
        rows = pl.ds(n * sub, sub)
        sc = lax.dot_general(q_ref[0, rows, :], kv, (((1,), (1,)), ((), ())), preferred_element_type=F32) * SCALE
        if first:
            at = pl.program_id(1) * tq + n * sub
            row = at + lax.broadcasted_iota(jnp.int32, sc.shape, 0)
            col = lax.broadcasted_iota(jnp.int32, sc.shape, 1)
            sc = jnp.where(row >= col, sc, -jnp.inf)
        new = jnp.max(sc, axis=-1, keepdims=True)
        if not first:
            old = m_ref[0, rows, :1]
            new = jnp.maximum(new, old)
            corr = jnp.exp(old - new)
        p = jnp.exp(sc - new)
        den = jnp.sum(p, axis=-1, keepdims=True)
        pv = jnp.dot(p.astype(BF16), kv[:, :r], preferred_element_type=F32)
        if not first:
            den = den + l_ref[0, rows, :1] * corr
            pv = pv + a_ref[0, rows, :] * corr
        mo_ref[0, rows, :] = jnp.broadcast_to(new, (sub, LANES))
        lo_ref[0, rows, :] = jnp.broadcast_to(den, (sub, LANES))
        ao_ref[0, rows, :] = pv


def _update(state, qc, kv, r):
    rows, heads, seq, e = qc.shape
    nh = rows * heads
    tq = min(512, seq)
    sub = min(256, tq)
    first = state is None
    stat = pl.BlockSpec((1, tq, LANES), lambda h, i: (h, i, 0))
    accs = pl.BlockSpec((1, tq, r), lambda h, i: (h, i, 0))
    return pl.pallas_call(
        functools.partial(_block_kernel, r, sub, first),
        grid=(nh, seq // tq),
        in_specs=[pl.BlockSpec((1, tq, e), lambda h, i: (h, i, 0)),
                  pl.BlockSpec((1, seq, e), lambda h, i: (h // heads, 0, 0))] + ([] if first else [stat, stat, accs]),
        out_specs=[stat, stat, accs],
        out_shape=[jax.ShapeDtypeStruct((nh, seq, LANES), F32), jax.ShapeDtypeStruct((nh, seq, LANES), F32),
                   jax.ShapeDtypeStruct((nh, seq, r), F32)],
        compiler_params=pltpu.CompilerParams(dimension_semantics=('arbitrary', 'arbitrary'), vmem_limit_bytes=48 * 2**20),
        cost_estimate=pl.CostEstimate(flops=2 * nh * seq * seq * (e + r), bytes_accessed=nh * seq * (2 * e + 8 * r),
                                      transcendentals=nh * seq * seq),
    )(qc.reshape(nh, seq, e), kv, *(() if first else state))


def _finish(state, w_uv, w_o):
    heads, r, vd = w_uv.shape
    _, den, acc = state
    seq = acc.shape[1]
    den = den[:, :, 0].reshape(-1, heads, seq)
    acc = acc.reshape(-1, heads, seq, r)
    lat = (acc / den[..., None]).astype(BF16)
    o = jnp.einsum('bhqr,hrv->bhqv', lat, w_uv, preferred_element_type=F32).astype(BF16)
    return jnp.einsum('cirw,iwe->cre', o, w_o.reshape(heads, vd, -1), preferred_element_type=F32).astype(BF16)


def _member(idt, first, n):
    e = first + jnp.arange(n, dtype=idt.dtype)
    return jnp.any(idt[..., :, None, :] == e[:, None], axis=-3)


def _ranks(hit):
    t = hit.shape[-1]
    k = jnp.arange(t)
    tri = (k[:, None] < k[None, :]).astype(BF16)
    flat = hit.reshape(-1, t)
    pre = jnp.dot(flat.astype(BF16), tri, preferred_element_type=F32).astype(jnp.int32)
    return jnp.where(flat, pre, -1).reshape(hit.shape)


def _expert(xs, wg, wu, wd):
    hid = jax.nn.silu(jnp.dot(xs, wg, preferred_element_type=F32)) * jnp.dot(xs, wu, preferred_element_type=F32)
    return jnp.dot(hid.astype(BF16), wd, preferred_element_type=F32).astype(BF16)


def _split(w):
    hi = w.astype(BF16)
    r1 = w - hi.astype(F32)
    mid = r1.astype(BF16)
    lo = (r1 - mid.astype(F32)).astype(BF16)
    return hi, mid, lo


def solution(mesh):
    ncp = mesh.shape['cp']
    ngroup = mesh.shape['b'] * ncp
    axes = ('b', 'cp')
    tok = P(('dp', 'b'), 'cp', None)
    rep = P()
    espec = P(('b', 'cp'), None, None)

    def body(x, ids, g_attn, w_q, w_dkv, w_kr, w_uk, w_uv, w_o, g_ffn, w_fg, w_fu, w_fd, g_moe, w_r, w_eg, w_eu, w_ed):
        rows, seq, d = x.shape
        heads, r, _ = w_uv.shape
        top = ids.shape[-1]
        t = rows * seq
        epd = w_eg.shape[0]
        ne = epd * ngroup
        hot = (w_r.shape[1] // top) // 2
        cap = (t + hot - 1) // hot
        i = lax.axis_index('cp')
        me = lax.axis_index('b') * ncp + i
        loc = jnp.arange(seq)
        slots = jnp.arange(cap, dtype=jnp.int32)
        u = _rms(x, g_moe).reshape(t, d)
        idt = ids.reshape(t, top).T
        idall = lax.all_gather(idt, axes, axis=0, tiled=False)
        uall = lax.all_gather(u, axes, axis=0, tiled=False)
        g = jax.nn.softmax(jnp.einsum('td,de->et', u, w_r, preferred_element_type=F32), axis=0)
        hit = _member(idt, 0, g.shape[0])
        sel = jnp.where(hit, g, 0.0)
        gate = sel / jnp.sum(sel, axis=0, keepdims=True)
        rank = _ranks(hit[:ne]).reshape(ngroup, epd, t).transpose(1, 2, 0)
        parts = _split(gate[:ne].reshape(ngroup, epd, t).transpose(1, 2, 0))
        m = jnp.sum(gate[ne:], axis=0)[:, None] * u.astype(F32)
        qc, kv = _prep(x, i * seq + loc, g_attn, w_q, w_dkv, w_kr, w_uk)
        state = _update(None, qc, kv, r)
        perm = [(k, (k + 1) % ncp) for k in range(ncp)]
        early = 1 + (ncp - 1) // 3
        cur = kv

        def attend(step, state, cur):
            cur = lax.ppermute(cur, 'cp', perm)
            state = lax.cond((i - step) % ncp < i,
                             lambda st, kb: tuple(_update(st, qc, kb, r)),
                             lambda st, kb: tuple(st), tuple(state), cur)
            return state, cur

        for step in range(1, min(early, ncp)):
            state, cur = attend(step, state, cur)
        rk = _ranks(_member(idall, me * epd, epd))
        (rk, uall, state, cur) = lax.optimization_barrier((rk, uall, state, cur))

        def chunk(k, src):
            pick = (rk[:, k, None, :] == slots[:, None]).astype(BF16)
            xs = jnp.einsum('sct,std->scd', pick, src, preferred_element_type=F32).astype(BF16)
            out = _expert(xs.reshape(ngroup * cap, d), w_eg[k], w_eu[k], w_ed[k])
            return out.reshape(ngroup, cap, d)

        def weights(k):
            on = rank[k][:, :, None] == slots
            w = jnp.stack([jnp.where(on, part[k][:, :, None].astype(F32), 0.0).astype(BF16) for part in parts])
            return w.reshape(len(parts), t, ngroup * cap)

        def add(m, w, ret):
            part = jnp.einsum('xtp,pd->xtd', w, ret.reshape(ngroup * cap, d), preferred_element_type=F32)
            return m + jnp.sum(part, axis=0)

        rets = []
        for k in range(epd):
            out = chunk(k, uall)
            rets.append(lax.all_to_all(out, axes, 0, 0))
            uall, rk, _ = lax.optimization_barrier((uall, rk, out))
        late = list(range(min(early, ncp), ncp))
        waits = iter(range(epd - 1))
        for step in late:
            k = next(waits, None)
            if k is not None:
                state, rets[k] = lax.optimization_barrier((state, rets[k]))
            state, cur = attend(step, state, cur)
        a = _finish(state, w_uv, w_o)
        y = (x.astype(F32) + a.astype(F32)).astype(BF16).reshape(t, d)
        z = _rms(y, g_ffn)
        for k in waits:
            z, rets[k] = lax.optimization_barrier((z, rets[k]))
        f = _swiglu(z, w_fg, w_fu, w_fd)
        for k in range(epd):
            m = add(m, weights(k), rets[k])
        h = y.astype(F32) + f.astype(F32) + m
        return h.astype(BF16).reshape(rows, seq, d)

    return jax.shard_map(body, mesh=mesh, in_specs=(tok, tok) + (rep,) * 13 + (espec,) * 3, out_specs=tok, check_vma=False)
```

time: 2080 us -> 1560 us (0.75)
  waiting for transfers between devices: 710 us -> 156 us
  Pallas kernels: 0 us -> 307 us
  matrix products: 936 us -> 717 us
  other arithmetic: 211 us -> 125 us
  blocking collectives: 0 us -> 52.5 us
  local copies, waits for them, and re-layouts: 195 us -> 154 us
    all_to_all x2 -> x4, waiting for transfers between devices: 710 us -> 156 us  [body(): rets.append(lax.all_to_all(out, axes, 0, 0))]
    pallas_call x0 -> x4, Pallas kernels: none -> 307 us  [_update(): pl.pallas_call(functools.partial(_block_kernel, r, sub, first), grid=(nh,...]
    dot_general x15 -> x19, matrix products: 690 us -> 468 us  [the longest x4 141 us: _expert(): jnp.dot(hid.astype(BF16), wd, preferred_element_type=F32).astype(BF16)]
    cond x2 -> x17, local copies, waits for them, and re-layouts: 0.01 us -> 108 us
    reduce_sum x8 -> x3, other arithmetic: 86.9 us -> 1.69 us  [the longest x1 1.5 us: body(): m = jnp.sum(gate[ne:], axis=0)[:, None] * u.astype(F32)]
    broadcast_in_dim x2 -> x0, local copies, waits for them, and re-layouts: 57.4 us -> none  [_route(): return (sel, jnp.where(sel, ge[:, :, None], 0.0))]
    all_gather x0 -> x1, blocking collectives: none -> 52.5 us  [body(): idall = lax.all_gather(idt, axes, axis=0, tiled=False)]
    eq x3 -> x0, local copies, waits for them, and re-layouts: 47.7 us -> none  [_route(): pre[:, :, None] == jnp.arange(cap, dtype=lab.dtype)]
  transfers between devices with their start and end apart: 5 -> 8, of which waited for: 1 -> 2; matrix products, arithmetic and copies ran while one was open for 52% -> 52% of each run, Pallas kernels for 0% -> 20%
where the time goes in v1:
time: 1560 us; the launch traced here: 1550 us
  matrix products  717 us (46%)
  Pallas kernels  307 us (20%)
  waiting for transfers between devices  156 us (10%)
  local copies, waits for them, and re-layouts  154 us (10%)
  other arithmetic  125 us (8%)
  blocking collectives  52.5 us (3%)
  starting transfers between devices  26.1 us (2%)
    pallas_call x4, Pallas kernels, _update(): pl.pallas_call(functools.partial(_block_kernel, r, sub, first), grid=(nh,...  307 us
    all_to_all x4, waiting for transfers between devices, body(): rets.append(lax.all_to_all(out, axes, 0, 0))  156 us
    dot_general x4, matrix products, _expert(): jnp.dot(hid.astype(BF16), wd, preferred_element_type=F32).astype(BF16)  141 us
    dot_general x4, matrix products, add(): jnp.einsum('xtp,pd->xtd', w, ret.reshape(ngroup * cap, d), preferred_elem...  138 us
    dot_general x4, matrix products, chunk(): jnp.einsum('sct,std->scd', pick, src, preferred_element_type=F32)  109 us
    cond x16, local copies, waits for them, and re-layouts  98.8 us
    dot_general x4, matrix products, _expert(): jnp.dot(xs, wg, preferred_element_type=F32)  74 us
    dot_general x1, matrix products, _swiglu(): jnp.dot(z, wu, preferred_element_type=F32)  63.4 us
  transfers between devices with their start and end apart: 8, of which 2 were waited for; matrix products, arithmetic and copies ran while one was open for 52% of the time, Pallas kernels for 20%

profile of v1, /device:TPU:15, one launch (start us, length us, event | category | flops | bytes accessed | tf_op | source)
XLA Modules:
  0.0 1551.6 jit_solution(14608217852476864077)
XLA Ops:
  7.4 3.1 fusion.30
  10.5 5.2 fusion.28
  15.9 3.6 fusion.132
  19.5 2.4 fusion.144
  22.0 2.4 fusion.129
  26.8 52.5 %all-gather.1 = s32[16,6,1024]{2,1,0:T(8,128)S(1)} all-gather(s32[1,6,1024]{2,1,0:T(8,128)S(1)} %bitcast.288), channel_id=2, replica_groups=mesh['dp'=2,'b'=4,'cp'=4] {'b','cp'}, dimensions={0}, use_global_device_ids=true | all-gather | bytes 417792 | tf_op jit(solution)/shard_map/all_gather | solution.py:168
  86.1 16.7 %copy.58 = bf16[2048,3072]{0,1:T(8,128)(2,1)} copy(bf16[2048,3072]{1,0:T(8,128)(2,1)} %param.27) | data formatting | bytes 25165824 | tf_op args[3]
  102.9 3.7 fusion.167
  125.9 2.5 multiply_cosine_fusion.1
  128.4 14.9 select_convert_fusion.2
  143.3 13.0 select_convert_fusion.5
  156.3 13.0 select_convert_fusion.8
  169.3 13.0 select_convert_fusion.11
  182.3 21.5 %convolution_bitcast_fusion = f32[1,1024,16,192]{3,1,2,0:T(8,128)} fusion(bf16[16,192,2048]{2,1,0:T(8,128)(2,1)S(1)} %bitcast.270, bf16[1,1024,2048]{2,1,0:T(8,128)(2,1)S(1)} %copy-done.7, f32[2048]{0:T(1024)S(1)} %convert_element_type.445, f32[1024]{0:T(1024)S(1)} %add_rsqrt_fusion.1), kind=kOutput, calls=%fused_computation.46 | convolution fusion | flops 12893290496 | bytes 29372416 | tf_op jit(solution)/shard_map/bsd,dk->bsk/dot_general | solution.py:45
  203.8 4.0 slice_bitcast_fusion
  207.8 5.0 subtract_convert_fusion
  212.8 11.6 convert_bitcast_fusion
  224.4 22.0 %fusion.194.q_ref = bf16[16,1024,576]{2,1,0:T(8,128)(2,1)} fusion(bf16[1,16,1024,32]{3,2,1,0:T(8,128)(2,1)} %get-tuple-element.180, bf16[1,16,1024,32]{3,2,1,0:T(8,128)(2,1)} %get-tuple-element.179, bf16[1,16,1024,512]{3,2,1,0:T(8,128)(2,1)} %convert_bitcast_fusion), kind=kLoop, calls=%fused_computation.236 | loop fusion | flops 56623104 | bytes 37748736 | tf_op jit(solution)/shard_map/reshape | solution.py:104
  246.4 69.6 %shard_map.172 = (f32[16,1024,128]{2,1,0:T(8,128)}, f32[16,1024,128]{2,1,0:T(8,128)}, f32[16,1024,512]{2,1,0:T(8,128)}) custom-call(bf16[16,1024,576]{2,1,0:T(8,128)(2,1)} %fusion.194.q_ref, bf16[1,1024,576]{2,1,0:T(8,128)(2,1)S(1)} %pad_maximum_fusion.1.kv_ref), custom_call_target="tpu_custom_call" | custom-call | flops 36507222016 | bytes 85983232 | tf_op jit(solution)/shard_map/pallas_call | solution.py:93
  316.0 19.6 %pad_maximum_fusion = bf16[1,16,1024,576]{3,2,1,0:T(8,128)(2,1)} fusion(bf16[1,16,1024,32]{3,2,1,0:T(8,128)(2,1)S(1)} %copy-done.5, bf16[1,16,1024,32]{3,2,1,0:T(8,128)(2,1)S(1)} %copy-done.4, bf16[1,16,1024,512]{3,2,1,0:T(8,128)(2,1)} %convert_bitcast_fusion), kind=kLoop, calls=%fused_computation.6 | loop fusion | flops 56623104 | bytes 37748736 | tf_op jit(solution)/shard_map/concatenate | solution.py:48
  335.6 115.1 %conditional.3 = ((f32[16,1024,128]{2,1,0:T(8,128)}, f32[16,1024,128]{2,1,0:T(8,128)}, f32[16,1024,512]{2,1,0:T(8,128)})) conditional(s32[]{:T(128)} %convert_element_type.444, (f32[16,1024,128]{2,1,0:T(8,128)}, f32[16,1024,128]{2,1,0:T(8,128)}, f32[16,1024,512]{2,1,0:T(8,128)}) %shard_map.172, (bf16[1,16,1024,576]{3,2,1,0:T(8,128)(2,1)}, ...), branch_computations={%region_2.0_spmd, %region_3.0_spmd} | conditional | flops 36507222016 | bytes 222560288 | solution.py:185
  337.4 7.6 copy.161.refs_0_
  345.0 3.3 copy.162.refs_1_
  348.3 23.0 %copy.163.refs_2_ = f32[16,1024,512]{2,1,0:T(8,128)} copy(f32[16,1024,512]{2,1,0:T(8,128)} %get-tuple-element.55) | data formatting | bytes 67108864 | tf_op jit(solution)/shard_map/cond
  371.3 79.4 %branch_1_fun.3 = (f32[16,1024,128]{2,1,0:T(8,128)}, f32[16,1024,128]{2,1,0:T(8,128)}, f32[16,1024,512]{2,1,0:T(8,128)}) custom-call(bf16[16,1024,576]{2,1,0:T(8,128)(2,1)} %bitcast.265, bf16[1,1024,576]{2,1,0:T(8,128)(2,1)S(1)} %copy.66.kv_ref, f32[16,1024,128]{2,1,0:T(8,128)} %copy.161.refs_0_, f32[16,1024,128]{2,1,0:T(8,128)} %copy.162.refs_1_, ...), custom_call_target="tpu_custom_call" | custom-call | flops 36507222016 | bytes 85983232 | tf_op jit(solution)/shard_map/cond/branch_1_fun/pallas_call | solution.py:93
  450.7 27.2 %fusion.88 = bf16[16,128,2048]{2,1,0:T(8,128)(2,1)} fusion(bf16[16,1024,2048]{2,1,0:T(8,128)(2,1)} %all-gather.4.cloned.1.call-done, s32[16,1024]{1,0:T(8,128)S(1)} %bitcast.284), kind=kOutput, calls=%fused_computation.128 | convolution fusion | flops 8596226048 | bytes 75563008 | tf_op jit(solution)/shard_map/sct,std->scd/dot_general | solution.py:197
  477.9 18.5 %fusion.63 = f32[2048,1408]{1,0:T(8,128)} fusion(bf16[2048,2048]{1,0:T(8,128)(2,1)} %bitcast.275, bf16[4,2048,1408]{2,1,0:T(8,128)(2,1)} %param.39), kind=kOutput, calls=%fused_computation.107 | convolution fusion | flops 11811160064 | bytes 25690112 | tf_op jit(solution)/shard_map/dot_general | solution.py:133
  496.4 35.2 %convolution_convert_fusion.3 = bf16[2048,2048]{1,0:T(8,128)(2,1)} fusion(f32[2048,1408]{1,0:T(8,128)} %fusion.63, bf16[2048,2048]{1,0:T(8,128)(2,1)} %bitcast.276, bf16[4,1408,2048]{2,1,0:T(8,128)(2,1)} %param.41, bf16[4,2048,1408]{2,1,0:T(8,128)(2,1)} %param.40), kind=kOutput, calls=%fused_computation.92 | convolution fusion | flops 23643815936 | bytes 39845888 | tf_op jit(solution)/shard_map/dot_general | solution.py:134
  531.7 8.6 all-to-all-start
  540.4 27.0 %fusion.87 = bf16[16,128,2048]{2,1,0:T(8,128)(2,1)} fusion(bf16[16,1024,2048]{2,1,0:T(8,128)(2,1)} %all-gather.4.cloned.1.call-done, s32[16,1024]{1,0:T(8,128)S(1)} %bitcast.285), kind=kOutput, calls=%fused_computation.127 | convolution fusion | flops 8596226048 | bytes 75563008 | tf_op jit(solution)/shard_map/sct,std->scd/dot_general | solution.py:197
  567.3 18.5 %fusion.58 = f32[2048,1408]{1,0:T(8,128)} fusion(bf16[2048,2048]{1,0:T(8,128)(2,1)} %bitcast.277, bf16[4,2048,1408]{2,1,0:T(8,128)(2,1)} %param.39), kind=kOutput, calls=%fused_computation.103 | convolution fusion | flops 11811160064 | bytes 25690112 | tf_op jit(solution)/shard_map/dot_general | solution.py:133
  585.8 35.2 %convolution_convert_fusion.2 = bf16[2048,2048]{1,0:T(8,128)(2,1)} fusion(f32[2048,1408]{1,0:T(8,128)} %fusion.58, bf16[2048,2048]{1,0:T(8,128)(2,1)} %bitcast.278, bf16[4,1408,2048]{2,1,0:T(8,128)(2,1)} %param.41, bf16[4,2048,1408]{2,1,0:T(8,128)(2,1)} %param.40), kind=kOutput, calls=%fused_computation.91 | convolution fusion | flops 23643815936 | bytes 39845888 | tf_op jit(solution)/shard_map/dot_general | solution.py:134
  621.1 27.4 %fusion.86 = bf16[16,128,2048]{2,1,0:T(8,128)(2,1)} fusion(bf16[16,1024,2048]{2,1,0:T(8,128)(2,1)} %all-gather.4.cloned.1.call-done, s32[16,1024]{1,0:T(8,128)S(1)} %bitcast.286), kind=kOutput, calls=%fused_computation.126 | convolution fusion | flops 8596226048 | bytes 75563008 | tf_op jit(solution)/shard_map/sct,std->scd/dot_general | solution.py:197
  648.5 74.2 %all-to-all-done = bf16[16,128,2048]{2,1,0:T(8,128)(2,1)} async-done(((bf16[16,128,2048]{2,1,0:T(8,128)(2,1)}), bf16[16,128,2048]{2,1,0:T(8,128)(2,1)}, u32[]{:S(2)}, u32[]{:S(2)}) %all-to-all-start) | async-done | bytes 8388640 | tf_op jit(solution)/shard_map/all_to_all | solution.py:213
  722.7 4.9 all-to-all-start.1
  727.6 18.5 %fusion.53 = f32[2048,1408]{1,0:T(8,128)} fusion(bf16[2048,2048]{1,0:T(8,128)(2,1)} %bitcast.273, bf16[4,2048,1408]{2,1,0:T(8,128)(2,1)} %param.39), kind=kOutput, calls=%fused_computation.99 | convolution fusion | flops 11811160064 | bytes 25690112 | tf_op jit(solution)/shard_map/dot_general | solution.py:133
  746.1 35.3 %convolution_convert_fusion.1 = bf16[2048,2048]{1,0:T(8,128)(2,1)} fusion(f32[2048,1408]{1,0:T(8,128)} %fusion.53, bf16[2048,2048]{1,0:T(8,128)(2,1)} %bitcast.274, bf16[4,1408,2048]{2,1,0:T(8,128)(2,1)} %param.41, bf16[4,2048,1408]{2,1,0:T(8,128)(2,1)} %param.40), kind=kOutput, calls=%fused_computation.90 | convolution fusion | flops 23643815936 | bytes 39845888 | tf_op jit(solution)/shard_map/dot_general | solution.py:134
  782.1 27.1 %fusion.85 = bf16[16,128,2048]{2,1,0:T(8,128)(2,1)} fusion(bf16[16,1024,2048]{2,1,0:T(8,128)(2,1)} %all-gather.4.cloned.1.call-done, s32[16,1024]{1,0:T(8,128)S(1)} %bitcast.283), kind=kOutput, calls=%fused_computation.125 | convolution fusion | flops 8596226048 | bytes 75563008 | tf_op jit(solution)/shard_map/sct,std->scd/dot_general | solution.py:197
  809.3 18.5 %fusion.48 = f32[2048,1408]{1,0:T(8,128)} fusion(bf16[2048,2048]{1,0:T(8,128)(2,1)} %bitcast.271, bf16[4,2048,1408]{2,1,0:T(8,128)(2,1)} %param.39), kind=kOutput, calls=%fused_computation.95 | convolution fusion | flops 11811160064 | bytes 25690112 | tf_op jit(solution)/shard_map/dot_general | solution.py:133
  827.9 82.3 %all-to-all-done.1 = bf16[16,128,2048]{2,1,0:T(8,128)(2,1)} async-done(((bf16[16,128,2048]{2,1,0:T(8,128)(2,1)}), bf16[16,128,2048]{2,1,0:T(8,128)(2,1)}, u32[]{:S(2)}, u32[]{:S(2)}) %all-to-all-start.1) | async-done | bytes 8388640 | tf_op jit(solution)/shard_map/all_to_all | solution.py:213
  910.2 4.8 all-to-all-start.2
  915.0 35.2 %convolution_convert_fusion = bf16[2048,2048]{1,0:T(8,128)(2,1)} fusion(f32[2048,1408]{1,0:T(8,128)} %fusion.48, bf16[2048,2048]{1,0:T(8,128)(2,1)} %bitcast.272, bf16[4,1408,2048]{2,1,0:T(8,128)(2,1)} %param.41, bf16[4,2048,1408]{2,1,0:T(8,128)(2,1)} %param.40), kind=kOutput, calls=%fused_computation.89 | convolution fusion | flops 23643815936 | bytes 39845888 | tf_op jit(solution)/shard_map/dot_general | solution.py:134
  950.2 115.1 %conditional.4 = ((f32[16,1024,128]{2,1,0:T(8,128)}, f32[16,1024,128]{2,1,0:T(8,128)}, f32[16,1024,512]{2,1,0:T(8,128)})) conditional(s32[]{:T(128)} %convert_element_type.440, (f32[16,1024,128]{2,1,0:T(8,128)}, f32[16,1024,128]{2,1,0:T(8,128)}, f32[16,1024,512]{2,1,0:T(8,128)}) %get-tuple-element.249, (bf16[1,16,1024,576]{3,2,1,0:T(8,128)(2,1)}, ...), branch_computations={%region_4.5_spmd, %region_5.6_spmd} | conditional | flops 36507222016 | bytes 222560288 | solution.py:185
  951.9 7.7 copy.164.refs_0_
  959.5 3.3 copy.165.refs_1_
  962.8 23.0 %copy.166.refs_2_ = f32[16,1024,512]{2,1,0:T(8,128)} copy(f32[16,1024,512]{2,1,0:T(8,128)} %get-tuple-element.60) | data formatting | bytes 67108864 | tf_op jit(solution)/shard_map/cond
  985.8 79.4 %branch_1_fun.4 = (f32[16,1024,128]{2,1,0:T(8,128)}, f32[16,1024,128]{2,1,0:T(8,128)}, f32[16,1024,512]{2,1,0:T(8,128)}) custom-call(bf16[16,1024,576]{2,1,0:T(8,128)(2,1)} %bitcast.266, bf16[1,1024,576]{2,1,0:T(8,128)(2,1)S(1)} %copy.67.kv_ref, f32[16,1024,128]{2,1,0:T(8,128)} %copy.164.refs_0_, f32[16,1024,128]{2,1,0:T(8,128)} %copy.165.refs_1_, ...), custom_call_target="tpu_custom_call" | custom-call | flops 36507222016 | bytes 85983232 | tf_op jit(solution)/shard_map/cond/branch_1_fun/pallas_call | solution.py:93
  1065.3 110.8 %conditional.5 = ((f32[16,1024,128]{2,1,0:T(8,128)}, f32[16,1024,512]{2,1,0:T(8,128)})) conditional(s32[]{:T(128)} %convert_element_type.439, (f32[16,1024,128]{2,1,0:T(8,128)}, f32[16,1024,512]{2,1,0:T(8,128)}) %tuple.37, (bf16[1,16,1024,576]{3,2,1,0:T(8,128)(2,1)}, bf16[1,1024,576]{1,2,0:T(8,128)(2,1)S(1)}, f32[16,1024,128]{2,1,0:T(8,128)}, ...), branch_computations={%region_6.7_spmd, %region_7.8_spmd} | conditional | flops 36507222016 | bytes 197394496 | solution.py:185
  1066.1 7.7 copy.167.refs_1_
  1073.8 23.3 %copy.168.refs_2_ = f32[16,1024,512]{2,1,0:T(8,128)} copy(f32[16,1024,512]{2,1,0:T(8,128)} %get-tuple-element.65) | data formatting | bytes 67108864 | tf_op jit(solution)/shard_map/cond
  1097.1 79.1 %branch_1_fun.5 = (f32[16,1024,128]{2,1,0:T(8,128)}, f32[16,1024,128]{2,1,0:T(8,128)}, f32[16,1024,512]{2,1,0:T(8,128)}) custom-call(bf16[16,1024,576]{2,1,0:T(8,128)(2,1)} %bitcast.267, bf16[1,1024,576]{2,1,0:T(8,128)(2,1)S(1)} %copy.68.kv_ref, f32[16,1024,128]{2,1,0:T(8,128)S(1)} %bitcast.264, f32[16,1024,128]{2,1,0:T(8,128)} %copy.167.refs_1_, ...), custom_call_target="tpu_custom_call" | custom-call | flops 36507222016 | bytes 85983232 | tf_op jit(solution)/shard_map/cond/branch_1_fun/pallas_call | solution.py:93
  1176.1 9.0 copy.69
  1186.0 15.1 fusion.124.clone.4
  1201.1 13.0 fusion.32
  1214.1 2.1 copy-done.10
  1216.2 3.0 fusion.34
  1219.2 6.3 all-to-all-start.3
  1225.5 55.2 %fusion.168 = f32[1024,11264]{1,0:T(8,128)} fusion(bf16[1024,2048]{1,0:T(8,128)(2,1)} %fusion.34, bf16[2048,11264]{1,0:T(8,128)(2,1)} %param.34), kind=kOutput, calls=%fused_computation.235 | convolution fusion | flops 47244640256 | bytes 96468992 | tf_op jit(solution)/shard_map/dot_general | solution.py:31
  1280.7 34.1 %bitcast_reduce_fusion.1 = f32[1024,2048]{1,0:T(8,128)} fusion(bf16[16,128,2048]{2,1,0:T(8,128)(2,1)} %all-to-all-done.2, bf16[1,1024,16,128]{3,1,2,0:T(8,128)(2,1)} %get-tuple-element.208, bf16[1,1024,16,128]{3,1,2,0:T(8,128)(2,1)} %get-tuple-element.209, bf16[1,1024,16,128]{3,1,2,0:T(8,128)(2,1)S(1)} %copy-done.8), kind=kOutput, calls=%fused_computation.3 | convolution fusion | flops 25786580992 | bytes 29360128 | tf_op jit(solution)/shard_map/xtp,pd->xtd/dot_general | solution.py:207
  1314.8 35.0 %bitcast_reduce_fusion.2 = f32[1024,2048]{1,0:T(8,128)} fusion(bf16[16,128,2048]{2,1,0:T(8,128)(2,1)} %all-to-all-done.1, bf16[1,1024,16,128]{3,1,2,0:T(8,128)(2,1)} %get-tuple-element.205, bf16[1,1024,16,128]{3,1,2,0:T(8,128)(2,1)} %get-tuple-element.206, bf16[1,1024,16,128]{3,1,2,0:T(8,128)(2,1)} %get-tuple-element.204), kind=kOutput, calls=%fused_computation.4 | convolution fusion | flops 25786580992 | bytes 29360128 | tf_op jit(solution)/shard_map/xtp,pd->xtd/dot_general | solution.py:207
  1349.8 34.0 %bitcast_reduce_fusion.3 = f32[1024,2048]{1,0:T(8,128)} fusion(bf16[16,128,2048]{2,1,0:T(8,128)(2,1)} %all-to-all-done, bf16[1,1024,16,128]{3,1,2,0:T(8,128)(2,1)} %get-tuple-element.202, bf16[1,1024,16,128]{3,1,2,0:T(8,128)(2,1)} %get-tuple-element.203, bf16[1,1024,16,128]{3,1,2,0:T(8,128)(2,1)S(1)} %copy-done.9), kind=kOutput, calls=%fused_computation.5 | convolution fusion | flops 25786580992 | bytes 29360128 | tf_op jit(solution)/shard_map/xtp,pd->xtd/dot_general | solution.py:207
  1383.8 63.4 %multiply_convert_fusion.clone.6 = bf16[1024,11264]{1,0:T(8,128)(2,1)} fusion(f32[1024,11264]{1,0:T(8,128)} %fusion.168, bf16[1024,2048]{1,0:T(8,128)(2,1)} %fusion.34, bf16[2048,11264]{1,0:T(8,128)(2,1)} %param.35), kind=kOutput, calls=%fused_computation.clone.clone.clone.clone.clone.1 | convolution fusion | flops 47313846272 | bytes 119537664 | tf_op jit(solution)/shard_map/dot_general | solution.py:31
  1447.2 34.6 %bitcast_reduce_fusion = f32[1024,2048]{1,0:T(8,128)} fusion(bf16[16,128,2048]{2,1,0:T(8,128)(2,1)} %all-to-all-done.3, bf16[1,1024,16,128]{3,1,2,0:T(8,128)(2,1)} %get-tuple-element.211, bf16[1,1024,16,128]{3,1,2,0:T(8,128)(2,1)} %get-tuple-element.212, bf16[1,1024,16,128]{3,1,2,0:T(8,128)(2,1)} %get-tuple-element.210), kind=kOutput, calls=%fused_computation.2 | convolution fusion | flops 25786580992 | bytes 29360128 | tf_op jit(solution)/shard_map/xtp,pd->xtd/dot_general | solution.py:207
  1481.8 62.7 %fusion.107 = bf16[1,1024,2048]{2,1,0:T(8,128)(2,1)} fusion(f32[1024,2048]{1,0:T(8,128)} %bitcast_reduce_fusion, f32[1024,2048]{1,0:T(8,128)} %bitcast_reduce_fusion.1, f32[1024,2048]{1,0:T(8,128)} %bitcast_reduce_fusion.2, f32[1024,2048]{1,0:T(8,128)} %bitcast_reduce_fusion.3, bf16[1024,2048]{1,0:T(8,128)(2,1)} %copy-done.10, ...), kind=kOutput, calls=%fused_computation.130 | convolution fusion | flops 47269806080 | bytes 115347456 | tf_op jit(solution)/shard_map/dot_general | solution.py:32
  (120 shorter events, 35.4 us)
Async XLA Ops:
  6.5 206.3 %copy-start = (bf16[16,128,512]{2,1,0:T(8,128)(2,1)S(1)}, bf16[16,128,512]{2,1,0:T(8,128)(2,1)}, u32[]{:S(2)}) copy-start(bf16[16,128,512]{2,1,0:T(8,128)(2,1)} %param.30) | copy-start | bytes 6291460
  6.5 444.2 %all-gather.4.cloned.1.call-start = ((), (), s32[]{:S(2)}) async-start(), calls=%async_computation.4 | async-start | bytes 71303168 | tf_op jit(solution)/shard_map/all_gather | solution.py:169
  7.4 8.4 copy-start.15
  7.4 8.5 copy-start.20
  15.8 6.1 copy-start.6
  15.8 6.1 copy-start.18
  15.8 8.5 copy-start.17
  21.9 4.9 copy-start.14
  26.0 309.6 %collective-permute-start = (bf16[1,1024,576]{1,2,0:T(8,128)(2,1)}, bf16[1,1024,576]{1,2,0:T(8,128)(2,1)}, u32[]{:S(2)}, u32[]{:S(2)}) collective-permute-start(bf16[1,1024,576]{1,2,0:T(8,128)(2,1)} %copy.65), channel_id=1, source_target_pairs={{0,1},{1,2},{2,3},{3,0},{4,5},{5,6},{6,7},{7,4},{8,9},{9,10},{10,1... | collective-permute-start | bytes 3538952 | tf_op jit(solution)/shard_map/ppermute | solution.py:184
  107.2 0.8 copy-start.11
  143.3 39.0 %slice-start.2 = ((s8[12582912]{0:T(1024)(128)(4,1)}), s8[4194304]{0:T(1024)(128)(4,1)S(1)}, s32[]{:S(2)}) async-start(s8[12582912]{0:T(1024)(128)(4,1)} %bitcast.268), calls=%async_computation.7 | async-start | bytes 8388608
  156.3 26.0 %slice-start.3 = ((s8[12582912]{0:T(1024)(128)(4,1)}), s8[4194304]{0:T(1024)(128)(4,1)S(1)}, s32[]{:S(2)}) async-start(s8[12582912]{0:T(1024)(128)(4,1)} %bitcast.268), calls=%async_computation.8 | async-start | bytes 8388608
  169.3 13.0 copy-start.7
  169.3 13.0 slice-start.4
  246.4 69.6 %copy-start.4 = (bf16[1,16,1024,32]{3,2,1,0:T(8,128)(2,1)S(1)}, bf16[1,16,1024,32]{3,2,1,0:T(8,128)(2,1)}, u32[]{:S(2)}) copy-start(bf16[1,16,1024,32]{3,2,1,0:T(8,128)(2,1)} %get-tuple-element.179) | copy-start | bytes 3145732
  246.4 69.6 %copy-start.5 = (bf16[1,16,1024,32]{3,2,1,0:T(8,128)(2,1)S(1)}, bf16[1,16,1024,32]{3,2,1,0:T(8,128)(2,1)}, u32[]{:S(2)}) copy-start(bf16[1,16,1024,32]{3,2,1,0:T(8,128)(2,1)} %get-tuple-element.180) | copy-start | bytes 3145732
  335.6 115.1 %slice-start.5 = ((s32[16,4,1024]{2,1,0:T(4,128)}), s32[16,1,1024]{2,1,0:T(1,128)S(1)}, s32[]{:S(2)}) async-start(s32[16,4,1024]{2,1,0:T(4,128)} %reshape.570), calls=%async_computation.10 | async-start | bytes 131072 | tf_op jit(solution)/shard_map/slice | solution.py:196
  337.3 7.6 copy-start.2
  531.7 8.6 copy-start.12
  531.7 191.0 %all-to-all-start = ((bf16[16,128,2048]{2,1,0:T(8,128)(2,1)}), bf16[16,128,2048]{2,1,0:T(8,128)(2,1)}, u32[]{:S(2)}, u32[]{:S(2)}) async-start(bf16[16,128,2048]{2,1,0:T(8,128)(2,1)} %bitcast.282), calls=%async_computation | async-start | bytes 16777216 | tf_op jit(solution)/shard_map/all_to_all | solution.py:213
  722.7 187.5 %all-to-all-start.1 = ((bf16[16,128,2048]{2,1,0:T(8,128)(2,1)}), bf16[16,128,2048]{2,1,0:T(8,128)(2,1)}, u32[]{:S(2)}, u32[]{:S(2)}) async-start(bf16[16,128,2048]{2,1,0:T(8,128)(2,1)} %bitcast.281), calls=%async_computation.1 | async-start | bytes 16777216 | tf_op jit(solution)/shard_map/all_to_all | solution.py:213
  781.5 46.3 %collective-permute-start.1 = (bf16[1,1024,576]{1,2,0:T(8,128)(2,1)}, bf16[1,1024,576]{1,2,0:T(8,128)(2,1)}, u32[]{:S(2)}, u32[]{:S(2)}) collective-permute-start(bf16[1,1024,576]{1,2,0:T(8,128)(2,1)} %collective-permute-done), channel_id=1, source_target_pairs={{0,1},{1,2},{2,3},{3,0},{4,5},{5,6},{6,7},{7,4},{8,9},{9,10},{10,1... | collective-permute-start | bytes 3538952 | tf_op jit(solution)/shard_map/ppermute | solution.py:184
  827.8 237.6 %collective-permute-start.2 = (bf16[1,1024,576]{1,2,0:T(8,128)(2,1)}, bf16[1,1024,576]{1,2,0:T(8,128)(2,1)S(1)}, u32[]{:S(2)}, u32[]{:S(2)}) collective-permute-start(bf16[1,1024,576]{1,2,0:T(8,128)(2,1)} %collective-permute-done.1), channel_id=1, source_target_pairs={{0,1},{1,2},{2,3},{3,0},{4,5},{5,6},{6,7},{7,4},{8,9},{9,10},{10,1... | collective-permute-start | bytes 3538952 | tf_op jit(solution)/shard_map/ppermute | solution.py:184
  910.2 309.0 %all-to-all-start.2 = ((bf16[16,128,2048]{2,1,0:T(8,128)(2,1)}), bf16[16,128,2048]{2,1,0:T(8,128)(2,1)}, u32[]{:S(2)}, u32[]{:S(2)}) async-start(bf16[16,128,2048]{2,1,0:T(8,128)(2,1)} %bitcast.279), calls=%async_computation.2 | async-start | bytes 16777216 | tf_op jit(solution)/shard_map/all_to_all | solution.py:213
  951.9 7.7 copy-start.3
  1066.1 31.0 %slice-start = ((s8[8388608]{0:T(1024)(128)(4,1)}), s8[4194304]{0:T(1024)(128)(4,1)S(1)}, s32[]{:S(2)}) async-start(s8[8388608]{0:T(1024)(128)(4,1)} %bitcast.263), calls=%async_computation.5 | async-start | bytes 8388608 | tf_op jit(solution)/shard_map/cond
  1073.8 23.3 %slice-start.1 = ((s8[8388608]{0:T(1024)(128)(4,1)}), s8[4194304]{0:T(1024)(128)(4,1)S(1)}, s32[]{:S(2)}) async-start(s8[8388608]{0:T(1024)(128)(4,1)} %bitcast.263), calls=%async_computation.6 | async-start | bytes 8388608 | tf_op jit(solution)/shard_map/cond
  1176.1 9.9 copy-start.19
  1201.1 15.1 copy-start.13
  1214.1 2.1 copy-start.10
  1219.2 228.0 %all-to-all-start.3 = ((bf16[16,128,2048]{2,1,0:T(8,128)(2,1)}), bf16[16,128,2048]{2,1,0:T(8,128)(2,1)}, u32[]{:S(2)}, u32[]{:S(2)}) async-start(bf16[16,128,2048]{2,1,0:T(8,128)(2,1)} %bitcast.280), calls=%async_computation.3 | async-start | bytes 16777216 | tf_op jit(solution)/shard_map/all_to_all | solution.py:213
  1225.5 55.2 %copy-start.8 = (bf16[1,1024,16,128]{3,1,2,0:T(8,128)(2,1)S(1)}, bf16[1,1024,16,128]{3,1,2,0:T(8,128)(2,1)}, u32[]{:S(2)}) copy-start(bf16[1,1024,16,128]{3,1,2,0:T(8,128)(2,1)} %get-tuple-element.207) | copy-start | bytes 12582916
  1314.8 35.0 %copy-start.9 = (bf16[1,1024,16,128]{3,1,2,0:T(8,128)(2,1)S(1)}, bf16[1,1024,16,128]{3,1,2,0:T(8,128)(2,1)}, u32[]{:S(2)}) copy-start(bf16[1,1024,16,128]{3,1,2,0:T(8,128)(2,1)} %get-tuple-element.201) | copy-start | bytes 12582916
  1447.2 34.6 %copy-start.16 = (f32[1024]{0:T(1024)S(1)}, f32[1024]{0:T(1024)}, u32[]{:S(2)}) copy-start(f32[1024]{0:T(1024)} %slice_reduce_fusion) | copy-start | bytes 12292
  1481.8 62.7 %copy-start.1 = (bf16[16,128,512]{2,1,0:T(8,128)(2,1)S(1)}, bf16[16,128,512]{2,1,0:T(8,128)(2,1)}, u32[]{:S(2)}) copy-start(bf16[16,128,512]{2,1,0:T(8,128)(2,1)} %param.30) | copy-start | bytes 6291460
Sparse Core Ops, SparseCore 0:
  15.9 329.5 all-gather.3
